TPU v7x, 32 devices: a whole 2x2x4 slice. The times are simulated.
32 devices in a mesh: member: 2 (over y), lat: 4 (over x, core), lon: 4 (over z).
Axes of the slice: x: 2, y: 2, z: 4, core: 2. Of those that a mesh axis runs over, the one named last changes fastest.
Arguments:
- field: bfloat16 [256, 512, 256], P(('member', 'lat'), 'lon'), parts along dimension 0, may hold values from -6 to 6
- mode_table: int32 [48], replicated, may hold values from 0 to 47, as said below
- analysis: bfloat16 [48, 48, 128], P(('lat', 'lon')), as said below
- synthesis: bfloat16 [48, 48, 128], P(('lat', 'lon')), as said below
- mixing: bfloat16 [1, 2, 256, 256], replicated, may hold values from -0.25 to 0.25
- degree_gain: float32 [1, 48, 256], replicated, may hold values from 0.25 to 1.75
- skip_weight: bfloat16 [1, 256, 256], replicated, may hold values from -0.375 to 0.375
Outputs:
- advanced: bfloat16 [256, 512, 256], P(('member', 'lat'), 'lon'), parts along dimension 0
- spectrum: bfloat16 [96, 48, 2, 256], P(('member', 'lat', 'lon')), parts along dimension 0
There are 2 independent parts, one for each index of `member`. A program takes and returns all parts, laid end to end along the dimension named above; an argument that names none is the same for every part. Nothing has to cross between parts.
Inputs may be any that keep to these rules, and one draw needn't show every extreme that they name: A permutation of 0 to 47; slot s of the spectral layout holds zonal wavenumber mode_table[s]. analysis[s, l, j] = weight[j] P(l, m, colat[j]) rounded to bfloat16, with m = mode_table[s], colat[j] = pi (j + 0.5) / 128, weight[j] = 2 pi^2 sin(colat[j]) / 65536, and P the orthonormal associated Legendre function of degree l and order m at cos(colat) without the Condon-Shortley phase, zero for l < m. synthesis[s, l, j] = c P(l, m, colat[j]) rounded to bfloat16, with m = mode_table[s], c = 1 where m = 0 and c = 2 elsewhere, P and colat as for analysis.
All inputs are finite; a program needn't handle non-finite values.
Results may differ from a plain program's by a relative error of at most 0.0062.
Values may be sent and summed in bfloat16 or wider, within the bound.
A program may use at most 64 MiB of HBM per device.

v0:
```python
import math

import jax
import jax.numpy as jnp
from jax import lax
from jax.sharding import PartitionSpec as P


def fourier_table(orders, length):
    phases = orders[:, None] * jnp.arange(length, dtype=jnp.int32)[None, :] % length
    angles = phases.astype(jnp.float32) * (2.0 * math.pi / length)
    return (
        jnp.stack([jnp.cos(angles), -jnp.sin(angles)], axis=1)
        .reshape(2 * orders.shape[0], length)
        .astype(jnp.bfloat16)
    )


def update(current, spectral, skip_matrix):
    shape_lead = current.shape
    direct = jnp.dot(
        current.reshape(-1, shape_lead[-1]), skip_matrix, preferred_element_type=jnp.float32
    ).reshape(shape_lead)
    pre_act = spectral.astype(jnp.float32) + direct
    return (current.astype(jnp.float32) + jax.nn.gelu(pre_act, approximate=False)).astype(
        jnp.bfloat16
    )


def per_device(field, mode_table, analysis, synthesis, mixing, degree_gain, skip_weight):
    lat_count = lax.axis_size("lat")
    lon_count = lax.axis_size("lon")
    lat_dev, lon_dev, channels = field.shape
    rows_full = lat_dev * lat_count
    points = lon_dev * lon_count
    mode_count = mode_table.shape[0]
    per_group = analysis.shape[0]
    forward = fourier_table(mode_table, points)
    mixed_last = None
    current = field
    row_block = lax.all_to_all(current, "lon", split_axis=0, concat_axis=1, tiled=True)
    lat_side = jnp.einsum(
        "rkc,qk->rqc", row_block, forward, preferred_element_type=jnp.float32
    ).astype(jnp.bfloat16)
    gathered = lax.all_to_all(lat_side, ("lat", "lon"), split_axis=1, concat_axis=0, tiled=True)
    lat_data = gathered.reshape(rows_full, per_group, 2 * channels)
    coefficients = jnp.einsum(
        "slj,jsx->slx", analysis, lat_data, preferred_element_type=jnp.float32
    ).astype(jnp.bfloat16)
    real_part = mixing[0, 0]
    imag_part = mixing[0, 1]
    joined = jnp.concatenate(
        [
            jnp.concatenate([real_part, imag_part], axis=1),
            jnp.concatenate([-imag_part, real_part], axis=1),
        ],
        axis=0,
    )
    product = jnp.dot(
        coefficients.reshape(-1, 2 * channels), joined, preferred_element_type=jnp.float32
    )
    product = product.reshape(per_group, mode_count, 2, channels)
    mixed_modes = (product * degree_gain[0][None, :, None, :]).astype(jnp.bfloat16)
    synthesized = jnp.einsum(
        "slj,slx->jsx",
        synthesis,
        mixed_modes.reshape(per_group, mode_count, 2 * channels),
        preferred_element_type=jnp.float32,
    )
    synthesized = synthesized.astype(jnp.bfloat16).reshape(rows_full, 2 * per_group, channels)
    returned = lax.all_to_all(synthesized, ("lat", "lon"), split_axis=0, concat_axis=1, tiled=True)
    spectral = jnp.einsum(
        "rqc,qk->rkc", returned, forward, preferred_element_type=jnp.float32
    ).astype(jnp.bfloat16)
    spectral, mixed_last = (spectral, mixed_modes)
    grid_part = lax.all_to_all(spectral, "lon", split_axis=1, concat_axis=0, tiled=True)
    current = update(current, grid_part, skip_weight[0])
    return (current, mixed_last)


def solution(mesh):
    in_specs = (
        P(("member", "lat"), "lon", None),
        P(),
        P(("lat", "lon"), None, None),
        P(("lat", "lon"), None, None),
        P(),
        P(),
        P(),
    )
    out_specs = (P(("member", "lat"), "lon", None), P(("member", "lat", "lon"), None, None, None))
    return jax.shard_map(
        per_device, mesh=mesh, in_specs=in_specs, out_specs=out_specs, check_vma=False
    )
```

profile of v0, /device:TPU:1, one launch (start us, length us, event | category | flops | bytes accessed | tf_op | source)
XLA Modules:
  0.0 160.6 jit_solution(3721329665403770944)
XLA Ops:
  0.6 0.0 copy-start
  0.6 0.0 copy-start.6
  0.7 5.6 %all-to-all-start = ((bf16[32,128,256]{2,1,0:T(8,128)(2,1)}), bf16[32,128,256]{2,1,0:T(8,128)(2,1)S(1)}, u32[]{:S(2)}, u32[]{:S(2)}) async-start(bf16[32,128,256]{2,1,0:T(8,128)(2,1)} %param.7), calls=%async_computation | async-start | bytes 4194304 | tf_op jit(solution)/shard_map/all_to_all | solution.py:41
  6.2 0.0 copy-done.6
  6.2 0.5 cosine_convert_fusion
  6.7 0.1 copy.50
  6.9 0.0 copy-start.2
  6.9 47.1 %all-to-all-done = bf16[32,128,256]{2,1,0:T(8,128)(2,1)S(1)} async-done(((bf16[32,128,256]{2,1,0:T(8,128)(2,1)}), bf16[32,128,256]{2,1,0:T(8,128)(2,1)S(1)}, u32[]{:S(2)}, u32[]{:S(2)}) %all-to-all-start) | async-done | bytes 2097184 | tf_op jit(solution)/shard_map/all_to_all | solution.py:41
  54.0 0.1 copy.51
  54.1 0.0 copy-start.3
  54.1 0.0 copy-start.4
  54.1 0.5 fusion.11
  54.6 0.0 copy-start.5
  54.6 1.0 copy.52
  55.6 5.1 %all-to-all-start.1 = ((bf16[8,96,256]{2,0,1:T(8,128)(2,1)}), bf16[8,96,256]{2,0,1:T(8,128)(2,1)S(1)}, u32[]{:S(2)}, u32[]{:S(2)}) async-start(bf16[8,96,256]{2,0,1:T(8,128)(2,1)} %copy.52), calls=%async_computation.1 | async-start | bytes 786432 | tf_op jit(solution)/shard_map/all_to_all | solution.py:45
  60.7 0.0 copy-done.2
  60.8 0.2 copy.55
  61.0 11.8 %all-to-all-done.1 = bf16[8,96,256]{2,0,1:T(8,128)(2,1)S(1)} async-done(((bf16[8,96,256]{2,0,1:T(8,128)(2,1)}), bf16[8,96,256]{2,0,1:T(8,128)(2,1)S(1)}, u32[]{:S(2)}, u32[]{:S(2)}) %all-to-all-start.1) | async-done | bytes 393248 | tf_op jit(solution)/shard_map/all_to_all | solution.py:45
  72.8 0.1 copy.53
  72.9 0.4 reshape.134
  73.3 0.0 copy-done.3
  73.3 0.0 copy-done.4
  73.3 0.4 fusion.12
  73.7 0.0 copy-done.5
  73.7 0.3 convolution_convert_fusion
  74.0 0.4 copy.57
  74.4 18.8 %all_to_all.60 = bf16[128,6,256]{2,1,0:T(8,128)(2,1)S(1)} all-to-all(bf16[128,6,256]{2,1,0:T(8,128)(2,1)S(1)} %copy.57), channel_id=1, replica_groups=mesh['member'=2,'lat'=4,'lon'=4] {'lat','lon'}, dimensions={0} | all-to-all | bytes 786432 | tf_op jit(solution)/shard_map/all_to_all | solution.py:71
  93.3 0.1 copy.59
  93.3 0.7 convert_bitcast_fusion
  94.1 2.5 %copy.61 = bf16[8,512,256]{2,0,1:T(8,128)(2,1)} copy(bf16[8,512,256]{2,1,0:T(8,128)(2,1)S(1)} %convert_bitcast_fusion) | data formatting | bytes 4194304 | tf_op jit(solution)/shard_map/convert_element_type | solution.py:74
  96.6 3.6 %all-to-all-start.3 = ((bf16[8,512,256]{2,0,1:T(8,128)(2,1)}), bf16[8,512,256]{2,0,1:T(8,128)(2,1)S(1)}, u32[]{:S(2)}, u32[]{:S(2)}) async-start(bf16[8,512,256]{2,0,1:T(8,128)(2,1)} %copy.61), calls=%async_computation.3 | async-start | bytes 4194304 | tf_op jit(solution)/shard_map/all_to_all | solution.py:76
  100.2 0.8 copy.56
  101.0 46.9 %all-to-all-done.3 = bf16[8,512,256]{2,0,1:T(8,128)(2,1)S(1)} async-done(((bf16[8,512,256]{2,0,1:T(8,128)(2,1)}), bf16[8,512,256]{2,0,1:T(8,128)(2,1)S(1)}, u32[]{:S(2)}, u32[]{:S(2)}) %all-to-all-start.3) | async-done | bytes 2097184 | tf_op jit(solution)/shard_map/all_to_all | solution.py:76
  147.9 0.0 copy-start.1
  147.9 0.6 copy.62
  148.5 0.0 copy-done
  148.5 1.0 copy-done.1
  149.5 11.1 %fusion.3 = bf16[32,128,256]{2,1,0:T(8,128)(2,1)} fusion(bf16[32,128,256]{2,1,0:T(8,128)(2,1)S(1)} %copy-done.1, f32[8,4,128,256]{3,2,0,1:T(8,128)S(1)} %copy.62, bf16[1,256,256]{2,1,0:T(8,128)(2,1)S(1)} %copy-done), kind=kOutput, calls=%fused_computation.4 | convolution fusion | flops 608174080 | bytes 8519680 | tf_op jit(solution)/shard_map/dot_general | solution.py:21
  (6 shorter events, 0.1 us)
Async XLA Ops:
  0.6 147.8 %copy-start = (bf16[1,256,256]{2,1,0:T(8,128)(2,1)S(1)}, bf16[1,256,256]{2,1,0:T(8,128)(2,1)}, u32[]{:S(2)}) copy-start(bf16[1,256,256]{2,1,0:T(8,128)(2,1)} %param.13) | copy-start | bytes 393220
  0.6 5.6 %copy-start.6 = (s32[48]{0:T(128)S(1)}, s32[48]{0:T(128)}, u32[]{:S(2)}) copy-start(s32[48]{0:T(128)} %param.8) | copy-start | bytes 580
  0.7 53.3 %all-to-all-start = ((bf16[32,128,256]{2,1,0:T(8,128)(2,1)}), bf16[32,128,256]{2,1,0:T(8,128)(2,1)S(1)}, u32[]{:S(2)}, u32[]{:S(2)}) async-start(bf16[32,128,256]{2,1,0:T(8,128)(2,1)} %param.7), calls=%async_computation | async-start | bytes 4194304 | tf_op jit(solution)/shard_map/all_to_all | solution.py:41
  6.9 53.8 %copy-start.2 = (bf16[1,2,256,256]{3,2,1,0:T(8,128)(2,1)S(1)}, bf16[1,2,256,256]{3,2,1,0:T(8,128)(2,1)}, u32[]{:S(2)}) copy-start(bf16[1,2,256,256]{3,2,1,0:T(8,128)(2,1)} %param.11) | copy-start | bytes 786436
  54.1 19.2 %copy-start.3 = (f32[1,48,256]{2,1,0:T(8,128)S(1)}, f32[1,48,256]{2,1,0:T(8,128)}, u32[]{:S(2)}) copy-start(f32[1,48,256]{2,1,0:T(8,128)} %param.12) | copy-start | bytes 147460
  54.1 19.2 %copy-start.4 = (bf16[3,48,128]{2,1,0:T(8,128)(2,1)S(1)}, bf16[3,48,128]{2,1,0:T(8,128)(2,1)}, u32[]{:S(2)}) copy-start(bf16[3,48,128]{2,1,0:T(8,128)(2,1)} %param.9) | copy-start | bytes 110596
  54.6 19.1 %copy-start.5 = (bf16[3,48,128]{2,1,0:T(8,128)(2,1)S(1)}, bf16[3,48,128]{2,1,0:T(8,128)(2,1)}, u32[]{:S(2)}) copy-start(bf16[3,48,128]{2,1,0:T(8,128)(2,1)} %param.10) | copy-start | bytes 110596
  55.6 17.2 %all-to-all-start.1 = ((bf16[8,96,256]{2,0,1:T(8,128)(2,1)}), bf16[8,96,256]{2,0,1:T(8,128)(2,1)S(1)}, u32[]{:S(2)}, u32[]{:S(2)}) async-start(bf16[8,96,256]{2,0,1:T(8,128)(2,1)} %copy.52), calls=%async_computation.1 | async-start | bytes 786432 | tf_op jit(solution)/shard_map/all_to_all | solution.py:45
  96.6 51.3 %all-to-all-start.3 = ((bf16[8,512,256]{2,0,1:T(8,128)(2,1)}), bf16[8,512,256]{2,0,1:T(8,128)(2,1)S(1)}, u32[]{:S(2)}, u32[]{:S(2)}) async-start(bf16[8,512,256]{2,0,1:T(8,128)(2,1)} %copy.61), calls=%async_computation.3 | async-start | bytes 4194304 | tf_op jit(solution)/shard_map/all_to_all | solution.py:76
  147.9 1.6 copy-start.1
where the time goes:
time: 162 us; the launch traced here: 161 us
  waiting for transfers between devices  106 us (65%)
  blocking collectives  18.8 us (12%)
  starting transfers between devices  14.2 us (9%)
  matrix products  13 us (8%)
  local copies, waits for them, and re-layouts  7.33 us (5%)
    all_to_all x1, waiting for transfers between devices, per_device(): lax.all_to_all(current, 'lon', split_axis=0, concat_axis=1, tiled=True)  47.1 us
    all_to_all x1, waiting for transfers between devices, per_device(): lax.all_to_all(spectral, 'lon', split_axis=1, concat_axis=0, tiled=True)  46.9 us
    all_to_all x1, blocking collectives, per_device(): lax.all_to_all(synthesized, ('lat', 'lon'), split_axis=0, concat_axis=1,...  18.8 us
    all_to_all x1, waiting for transfers between devices, per_device(): lax.all_to_all(lat_side, ('lat', 'lon'), split_axis=1, concat_axis=0, til...  11.8 us
    dot_general x1, matrix products, update(): jnp.dot(current.reshape(-1, shape_lead[-1]), skip_matrix, preferred_eleme...  11.1 us
    all_to_all x1, starting transfers between devices, per_device(): lax.all_to_all(current, 'lon', split_axis=0, concat_axis=1, tiled=True)  5.55 us
    all_to_all x1, starting transfers between devices, per_device(): lax.all_to_all(lat_side, ('lat', 'lon'), split_axis=1, concat_axis=0, til...  5.07 us
    all_to_all x1, starting transfers between devices, per_device(): lax.all_to_all(spectral, 'lon', split_axis=1, concat_axis=0, tiled=True)  3.61 us
  transfers between devices with their start and end apart: 3, of which 3 were waited for; matrix products, arithmetic and copies ran while one was open for 1% of the time, Pallas kernels for 0%

commit v1 on v0

v1 whole, which is shorter than its diff:
```python
import functools
import math

import jax
import jax.numpy as jnp
from jax import lax
from jax.experimental import pallas as pl
from jax.experimental.pallas import tpu as pltpu
from jax.sharding import PartitionSpec as P

ROWS = 16
PITCH = 20
LANES = 128


def fourier_table(orders, first, count, length):
    points = first + jnp.arange(count, dtype=jnp.int32)
    phases = orders[:, None] * points[None, :] % length
    angles = phases.astype(jnp.float32) * (2.0 * math.pi / length)
    return (
        jnp.stack([jnp.cos(angles), -jnp.sin(angles)], axis=1)
        .reshape(2 * orders.shape[0], count)
        .astype(jnp.bfloat16)
    )


def dot(a, b):
    return jnp.dot(a, b, preferred_element_type=jnp.float32)


def dot_t(a, b):
    return lax.dot_general(a, b, (((0,), (0,)), ((), ())), preferred_element_type=jnp.float32)


def spectral_kernel(
    lat_n, lon_n,
    field, table, analysis, synthesis, mixing, gain,
    mixed, returned,
    field_v, wide, outgoing, incoming, made, load_sem, own_sem, send_sem, recv_sem, back_send, back_recv,
):
    lat = lax.axis_index("lat")
    lon = lax.axis_index("lon")
    me = lat * lon_n + lon
    rows, points, channels = field_v.shape
    slots, degrees, _ = analysis.shape
    per = 2 * slots
    offsets = [(a, b) for b in range(lon_n) for a in range(lat_n) if a or b]
    halves = channels // LANES
    blocks = rows // ROWS
    queries = table.shape[0]

    loads = []
    for b in range(blocks):
        part = pl.ds(b * ROWS, ROWS)
        load = pltpu.make_async_copy(field.at[part], field_v.at[part], load_sem.at[b])
        load.start()
        loads.append(load)
    barrier = pltpu.get_barrier_semaphore()

    def peer(a, b):
        return lax.rem(lat + a, lat_n), lax.rem(lon + b, lon_n)

    for a, b in offsets:
        to_lat, to_lon = peer(a, b)
        pl.semaphore_signal(
            barrier, inc=1, device_id={"lat": to_lat, "lon": to_lon}, device_id_type=pl.DeviceIdType.MESH
        )

    transform = table[...]
    for b in range(blocks):
        loads[b].wait()

        @pl.loop(0, ROWS)
        def _(j):
            y = dot(transform, field_v[b * ROWS + j])
            for h in range(halves):
                wide.at[h][pl.ds(j, queries, stride=PITCH), :] = y[:, h * LANES : (h + 1) * LANES]

        @pl.loop(0, queries // 2)
        def _(i):
            base = pl.multiple_of(i * (2 * PITCH), 8)
            for h in range(halves):
                both = wide[h, pl.ds(base, 2 * PITCH), :]
                for u in range(2):
                    outgoing[2 * i + u, b * ROWS : (b + 1) * ROWS, h * LANES : (h + 1) * LANES] = both[
                        u * PITCH : u * PITCH + ROWS
                    ].astype(jnp.bfloat16)

    pl.semaphore_wait(barrier, len(offsets))
    place = lon * lat_n + lat
    sends = []
    for n, (a, b) in enumerate(offsets):
        to_lat, to_lon = peer(a, b)
        copy = pltpu.make_async_remote_copy(
            src_ref=outgoing.at[pl.ds((to_lat * lon_n + to_lon) * per, per)],
            dst_ref=incoming.at[:, place],
            send_sem=send_sem.at[n],
            recv_sem=recv_sem.at[n],
            device_id={"lat": to_lat, "lon": to_lon},
            device_id_type=pl.DeviceIdType.MESH,
        )
        copy.start()
        sends.append(copy)
    own = pltpu.make_async_copy(outgoing.at[pl.ds(me * per, per)], incoming.at[:, place], own_sem)
    own.start()
    own.wait()
    for copy in sends:
        copy.wait_recv()

    real_w = mixing[0]
    imag_w = mixing[1]
    gains = gain[...]
    all_rows = lat_n * rows
    for s in range(slots):
        weights = analysis[s]
        parts = []
        for r in range(2):
            acc = None
            for b in range(lon_n):
                lat_data = incoming[2 * s + r, b * lat_n : (b + 1) * lat_n].reshape(all_rows, channels)
                term = dot(weights, lat_data)
                acc = term if acc is None else acc + term
            parts.append(acc.astype(jnp.bfloat16))
        real = (dot(parts[0], real_w) - dot(parts[1], imag_w)) * gains
        imag = (dot(parts[0], imag_w) + dot(parts[1], real_w)) * gains
        both = [real.astype(jnp.bfloat16), imag.astype(jnp.bfloat16)]
        for r in range(2):
            mixed[s, :, r * channels : (r + 1) * channels] = both[r]
            made[2 * s + r] = (
                dot_t(synthesis[s], both[r]).astype(jnp.bfloat16).reshape(lat_n, rows, channels)
            )

    backs = []
    spot = pl.ds(me * per, per)
    for n, (a, b) in enumerate(offsets):
        to_lat, to_lon = peer(a, b)
        copy = pltpu.make_async_remote_copy(
            src_ref=made.at[:, to_lat],
            dst_ref=returned.at[spot],
            send_sem=back_send.at[n],
            recv_sem=back_recv.at[n],
            device_id={"lat": to_lat, "lon": to_lon},
            device_id_type=pl.DeviceIdType.MESH,
        )
        copy.start()
        backs.append(copy)
    own = pltpu.make_async_copy(made.at[:, lat], returned.at[spot], own_sem)
    own.start()
    own.wait()
    for copy in sends:
        copy.wait_send()
    for copy in backs:
        copy.wait()


def gelu(x):
    return 0.5 * x * (1.0 + lax.erf(x * math.sqrt(0.5)))


def grid_kernel(field, returned, table_t, skip, out, wide):
    rows, points, channels = field.shape
    queries = returned.shape[0]
    halves = channels // LANES

    @pl.loop(0, queries // 2)
    def _(i):
        base = pl.multiple_of(i * (2 * PITCH), 8)
        for u in range(2):
            row = returned[2 * i + u].astype(jnp.float32)
            for h in range(halves):
                wide[h, pl.ds(base + u * PITCH, ROWS), :] = row[:, h * LANES : (h + 1) * LANES]

    transform = table_t[...]
    weights = skip[...]

    @pl.loop(0, ROWS)
    def _(j):
        parts = [wide.at[h][pl.ds(j, queries, stride=PITCH), :] for h in range(halves)]
        values = jnp.concatenate(parts, axis=1).astype(jnp.bfloat16)
        spectral = dot(transform, values).astype(jnp.bfloat16).astype(jnp.float32)
        state = field[j]
        pre = spectral + dot(state, weights)
        out[j] = (state.astype(jnp.float32) + gelu(pre)).astype(jnp.bfloat16)


def per_device(lat_n, lon_n, field, mode_table, analysis, synthesis, mixing, degree_gain, skip_weight):
    rows, points, channels = field.shape
    modes = mode_table.shape[0]
    slots, degrees, all_rows = analysis.shape
    peers = lat_n * lon_n - 1
    queries = 2 * modes
    table = fourier_table(mode_table, lax.axis_index("lon") * points, points, points * lon_n)
    vmem = pl.BlockSpec(memory_space=pltpu.VMEM)
    anywhere = pl.BlockSpec(memory_space=pl.ANY)
    halves = channels // LANES
    mixed, returned = pl.pallas_call(
        functools.partial(spectral_kernel, lat_n, lon_n),
        out_shape=(
            jax.ShapeDtypeStruct((slots, degrees, 2 * channels), jnp.bfloat16),
            jax.ShapeDtypeStruct((queries, rows, channels), jnp.bfloat16),
        ),
        in_specs=[anywhere] + [vmem] * 5,
        out_specs=(vmem, anywhere),
        scratch_shapes=[
            pltpu.VMEM((rows, points, channels), jnp.bfloat16),
            pltpu.VMEM((halves, queries * PITCH, LANES), jnp.float32),
            pltpu.VMEM((queries, rows, channels), jnp.bfloat16),
            pltpu.VMEM((2 * slots, peers + 1, rows, channels), jnp.bfloat16),
            pltpu.VMEM((2 * slots, lat_n, rows, channels), jnp.bfloat16),
            pltpu.SemaphoreType.DMA((rows // ROWS,)),
            pltpu.SemaphoreType.DMA,
            pltpu.SemaphoreType.DMA((peers,)),
            pltpu.SemaphoreType.DMA((peers,)),
            pltpu.SemaphoreType.DMA((peers,)),
            pltpu.SemaphoreType.DMA((peers,)),
        ],
        compiler_params=pltpu.CompilerParams(
            collective_id=0, has_side_effects=True, vmem_limit_bytes=60 * 1024 * 1024
        ),
    )(field, table, analysis, synthesis, mixing[0], degree_gain[0])
    advanced = pl.pallas_call(
        grid_kernel,
        grid=(rows // ROWS,),
        out_shape=jax.ShapeDtypeStruct(field.shape, jnp.bfloat16),
        in_specs=[
            pl.BlockSpec((ROWS, points, channels), lambda i: (i, 0, 0)),
            pl.BlockSpec((queries, ROWS, channels), lambda i: (0, i, 0)),
            pl.BlockSpec((points, queries), lambda i: (0, 0)),
            pl.BlockSpec((channels, channels), lambda i: (0, 0)),
        ],
        out_specs=pl.BlockSpec((ROWS, points, channels), lambda i: (i, 0, 0)),
        scratch_shapes=[pltpu.VMEM((halves, queries * PITCH, LANES), jnp.float32)],
        compiler_params=pltpu.CompilerParams(vmem_limit_bytes=60 * 1024 * 1024),
    )(field, returned, table.T, skip_weight[0])
    return advanced, mixed.reshape(slots, degrees, 2, channels)


def solution(mesh):
    in_specs = (
        P(("member", "lat"), "lon", None),
        P(),
        P(("lat", "lon"), None, None),
        P(("lat", "lon"), None, None),
        P(),
        P(),
        P(),
    )
    out_specs = (P(("member", "lat"), "lon", None), P(("member", "lat", "lon"), None, None, None))
    body = functools.partial(per_device, mesh.shape["lat"], mesh.shape["lon"])
    return jax.shard_map(body, mesh=mesh, in_specs=in_specs, out_specs=out_specs, check_vma=False)
```

time: 162 us -> 98.3 us (0.61)
  the two profiles are of different devices: /device:TPU:1 before, /device:TPU:28 now
where the time goes in v1:
time: 98.3 us; the launch traced here: 98.2 us
  Pallas kernels  94.3 us (96%)
  local copies, waits for them, and re-layouts  2.35 us (2%)
    pallas_call x1, Pallas kernels, per_device(): pl.pallas_call(functools.partial(spectral_kernel, lat_n, lon_n), out_shap...  84.5 us
    pallas_call x1, Pallas kernels, per_device(): pl.pallas_call(grid_kernel, grid=(rows // ROWS,), out_shape=jax.ShapeDtyp...  9.74 us

profile of v1, /device:TPU:28, one launch (start us, length us, event | category | flops | bytes accessed | tf_op | source)
XLA Modules:
  0.0 98.2 jit_solution(2880272148488167216)
XLA Ops:
  0.6 0.8 cosine_convert_fusion
  1.5 0.0 copy-start
  1.5 0.7 copy.12
  2.3 0.0 copy-done
  2.3 84.5 %shard_map.86 = (bf16[3,48,512]{2,1,0:T(8,128)(2,1)}, bf16[96,32,256]{2,1,0:T(8,128)(2,1)}) custom-call(bf16[32,128,256]{2,1,0:T(8,128)(2,1)} %field.3, bf16[96,128]{1,0:T(8,128)(2,1)} %bitcast.7, bf16[3,48,128]{2,1,0:T(8,128)(2,1)} %analysis.1, bf16[3,48,128]{2,1,0:T(8,128)(2,1)} %synthesis.1, bf16[2,256,256]{2,1,0:T(8,128)(2,1)} %bitcast.5, f32[48,256]{1,0:T(8,128)} %bitcast.10), custom_call_target="tpu_custom_call" | custom-call | tf_op jit(solution)/shard_map/pallas_call | solution.py:196
  86.8 1.6 %reshape.134 = bf16[3,48,2,256]{3,2,1,0:T(2,128)(2,1)} reshape(bf16[3,48,512]{2,1,0:T(8,128)(2,1)} %get-tuple-element.5) | data formatting | bytes 294912 | tf_op jit(solution)/shard_map/reshape | solution.py:235
  88.4 9.7 %shard_map.87 = bf16[32,128,256]{2,1,0:T(8,128)(2,1)} custom-call(bf16[32,128,256]{2,1,0:T(8,128)(2,1)} %field.3, bf16[96,32,256]{2,1,0:T(8,128)(2,1)} %get-tuple-element.4.returned, bf16[128,96]{1,0:T(8,128)(2,1)} %bitcast.8, bf16[256,256]{1,0:T(8,128)(2,1)} %bitcast.9), custom_call_target="tpu_custom_call" | custom-call | tf_op jit(solution)/shard_map/pallas_call | solution.py:221
  (3 shorter events, 0.0 us)
Async XLA Ops:
  1.5 0.7 copy-start

commit v2 on v1

--- a/solution.py
+++ b/solution.py
@@ -11,6 +11,7 @@
 ROWS = 16
 PITCH = 20
 LANES = 128
+VMEM_BYTES = 60 * 1024 * 1024
 
 
 def fourier_table(orders, first, count, length):
@@ -153,6 +154,176 @@
         copy.wait()
 
 
+def staged_kernel(
+    lat_n, lon_n,
+    field, table, analysis, synthesis, mixing, gain,
+    mixed, returned,
+    field_v, wide, outgoing, gathered, analysis_all, synthesis_all, part_out, part_in, mixed_all, made,
+    load_sem, own_sem, table_send, table_recv, lat_send, lat_recv, lon_send, lon_recv,
+    mix_send, mix_recv, back_send, back_recv,
+):
+    lat = lax.axis_index("lat")
+    lon = lax.axis_index("lon")
+    rows, points, channels = field_v.shape
+    slots, degrees, _ = analysis.shape
+    per = 2 * slots
+    all_rows = lat_n * rows
+    order = list(range(1, lon_n))[::-1] + [0]
+
+    def at_lat(a):
+        return lax.rem(lat + a, lat_n)
+
+    def at_lon(b):
+        return lax.rem(lon + b + lon_n, lon_n)
+
+    def remote(src, dst, send, recv, to_lat, to_lon):
+        copy = pltpu.make_async_remote_copy(
+            src_ref=src, dst_ref=dst, send_sem=send, recv_sem=recv,
+            device_id={"lat": to_lat, "lon": to_lon}, device_id_type=pl.DeviceIdType.MESH,
+        )
+        copy.start()
+        return copy
+
+    loads = []
+    for b in range(rows // ROWS):
+        part = pl.ds(b * ROWS, ROWS)
+        load = pltpu.make_async_copy(field.at[part], field_v.at[part], load_sem.at[b])
+        load.start()
+        loads.append(load)
+    barrier = pltpu.get_barrier_semaphore()
+    peers = [(at_lat(a), lon) for a in range(1, lat_n)] + [(lat, at_lon(b)) for b in range(1, lon_n)]
+    for to_lat, to_lon in peers:
+        pl.semaphore_signal(
+            barrier, inc=1, device_id={"lat": to_lat, "lon": to_lon}, device_id_type=pl.DeviceIdType.MESH
+        )
+
+    tables = []
+    transform = table[...]
+    for b in range(rows // ROWS):
+        loads[b].wait()
+        forward_rows(transform, field_v, wide, b)
+        if b == 0:
+            pl.semaphore_wait(barrier, len(peers))
+            for k in range(1, lon_n):
+                for t, (src, dst) in enumerate(((analysis, analysis_all), (synthesis, synthesis_all))):
+                    tables.append(
+                        remote(src, dst.at[k], table_send.at[t, k], table_recv.at[t, k], lat, at_lon(-k))
+                    )
+        relay_rows(wide, outgoing, b, lat_n, lon_n, per)
+
+    lat_copies = {}
+    for b in order:
+        target = at_lon(b)
+        own = pltpu.make_async_copy(outgoing.at[lat, target], gathered.at[b, :, lat], own_sem.at[b])
+        copies = [
+            remote(
+                outgoing.at[at_lat(a), target], gathered.at[b, :, lat],
+                lat_send.at[b, a], lat_recv.at[b, a], at_lat(a), lon,
+            )
+            for a in range(1, lat_n)
+        ]
+        own.start()
+        lat_copies[b] = (own, copies)
+
+    lon_copies = []
+    kept = []
+    for b in order:
+        own, copies = lat_copies[b]
+        own.wait()
+        for copy in copies:
+            copy.wait_recv()
+        if b:
+            tables[2 * (b - 1)].wait_recv()
+        for s in range(slots):
+            weights = analysis_all[b, s] if b else analysis[s]
+            for r in range(2):
+                value = dot(weights, gathered[b, 2 * s + r].reshape(all_rows, channels))
+                if b:
+                    part_out[b, s, :, r * channels : (r + 1) * channels] = value.astype(jnp.bfloat16)
+                else:
+                    kept.append(value)
+        if b:
+            lon_copies.append(
+                remote(part_out.at[b], part_in.at[b], lon_send.at[b], lon_recv.at[b], lat, at_lon(b))
+            )
+    for copy in lon_copies:
+        copy.wait_recv()
+
+    real_w = mixing[0]
+    imag_w = mixing[1]
+    gains = gain[...]
+    for s in range(slots):
+        parts = []
+        for r in range(2):
+            total = kept[2 * s + r]
+            for b in range(1, lon_n):
+                total = total + part_in[b, s, :, r * channels : (r + 1) * channels].astype(jnp.float32)
+            parts.append(total.astype(jnp.bfloat16))
+        real = (dot(parts[0], real_w) - dot(parts[1], imag_w)) * gains
+        imag = (dot(parts[0], imag_w) + dot(parts[1], real_w)) * gains
+        mixed[s, :, :channels] = real.astype(jnp.bfloat16)
+        mixed[s, :, channels:] = imag.astype(jnp.bfloat16)
+
+    mix_copies = {
+        b: remote(mixed, mixed_all.at[b], mix_send.at[b], mix_recv.at[b], lat, at_lon(-b))
+        for b in range(1, lon_n)
+    }
+    backs = []
+    owns = []
+    for b in range(lon_n):
+        if b:
+            mix_copies[b].wait_recv()
+            tables[2 * (b - 1) + 1].wait_recv()
+        for s in range(slots):
+            weights = synthesis_all[b, s] if b else synthesis[s]
+            values = dot_t(weights, mixed_all[b, s] if b else mixed[s]).astype(jnp.bfloat16)
+            for r in range(2):
+                for a in range(lat_n):
+                    made[a, b, 2 * s + r] = values[a * rows : (a + 1) * rows, r * channels : (r + 1) * channels]
+        spot = pl.ds((lat * lon_n + at_lon(b)) * per, per)
+        for a in range(1, lat_n):
+            backs.append(
+                remote(
+                    made.at[at_lat(a), b], returned.at[spot],
+                    back_send.at[b, a], back_recv.at[b, a], at_lat(a), lon,
+                )
+            )
+        own = pltpu.make_async_copy(made.at[lat, b], returned.at[spot], own_sem.at[b])
+        own.start()
+        owns.append(own)
+    for own in owns:
+        own.wait()
+    for copy in tables + [c for b in order for c in lat_copies[b][1]] + lon_copies + list(mix_copies.values()):
+        copy.wait_send()
+    for copy in backs:
+        copy.wait()
+
+
+def forward_rows(transform, field_v, wide, b):
+    queries = transform.shape[0]
+
+    @pl.loop(0, ROWS, unroll=2)
+    def _(j):
+        y = dot(transform, field_v[b * ROWS + j])
+        for h in range(wide.shape[0]):
+            wide.at[h][pl.ds(j, queries, stride=PITCH), :] = y[:, h * LANES : (h + 1) * LANES]
+
+
+def relay_rows(wide, outgoing, b, lat_n, lon_n, per):
+    @pl.loop(0, lat_n * lon_n)
+    def _(d):
+        a = d // lon_n
+        k = lax.rem(d, lon_n)
+        for i in range(per // 2):
+            base = pl.multiple_of((d * (per // 2) + i) * (2 * PITCH), 8)
+            for h in range(wide.shape[0]):
+                both = wide[h, pl.ds(base, 2 * PITCH), :]
+                for u in range(2):
+                    outgoing[
+                        a, k, 2 * i + u, b * ROWS : (b + 1) * ROWS, h * LANES : (h + 1) * LANES
+                    ] = both[u * PITCH : u * PITCH + ROWS].astype(jnp.bfloat16)
+
+
 def gelu(x):
     return 0.5 * x * (1.0 + lax.erf(x * math.sqrt(0.5)))
 
@@ -173,7 +344,7 @@
     transform = table_t[...]
     weights = skip[...]
 
-    @pl.loop(0, ROWS)
+    @pl.loop(0, ROWS, unroll=2)
     def _(j):
         parts = [wide.at[h][pl.ds(j, queries, stride=PITCH), :] for h in range(halves)]
         values = jnp.concatenate(parts, axis=1).astype(jnp.bfloat16)
@@ -193,29 +364,62 @@
     vmem = pl.BlockSpec(memory_space=pltpu.VMEM)
     anywhere = pl.BlockSpec(memory_space=pl.ANY)
     halves = channels // LANES
+    wide = pltpu.VMEM((halves, queries * PITCH, LANES), jnp.float32)
+    exchanged = (lat_n, lon_n, 2 * slots, rows, channels)
+    coded = (lon_n, slots, degrees, 2 * channels)
+    weights = (lon_n,) + analysis.shape
+    staged = [
+        ((rows, points, channels), jnp.bfloat16),
+        (exchanged, jnp.bfloat16),
+        ((lon_n, 2 * slots, lat_n, rows, channels), jnp.bfloat16),
+        (weights, jnp.bfloat16),
+        (weights, jnp.bfloat16),
+        (coded, jnp.bfloat16),
+        (coded, jnp.bfloat16),
+        (coded, jnp.bfloat16),
+        (exchanged, jnp.bfloat16),
+    ]
+    held = sum(2 * math.prod(shape) for shape, _ in staged) + 4 * halves * queries * PITCH * LANES
+    dma = pltpu.SemaphoreType.DMA
+    if held < VMEM_BYTES * 3 // 4:
+        kernel = staged_kernel
+        buffers = [pltpu.VMEM(shape, dtype) for shape, dtype in staged]
+        scratch = [buffers[0], wide] + buffers[1:] + [
+            dma((rows // ROWS,)),
+            dma((lon_n,)),
+            dma((2, lon_n)),
+            dma((2, lon_n)),
+            dma((lon_n, lat_n)),
+            dma((lon_n, lat_n)),
+            dma((lon_n,)),
+            dma((lon_n,)),
+            dma((lon_n,)),
+            dma((lon_n,)),
+            dma((lon_n, lat_n)),
+            dma((lon_n, lat_n)),
+        ]
+    else:
+        kernel = spectral_kernel
+        scratch = [
+            pltpu.VMEM((rows, points, channels), jnp.bfloat16),
+            wide,
+            pltpu.VMEM((queries, rows, channels), jnp.bfloat16),
+            pltpu.VMEM((2 * slots, peers + 1, rows, channels), jnp.bfloat16),
+            pltpu.VMEM((2 * slots, lat_n, rows, channels), jnp.bfloat16),
+            dma((rows // ROWS,)),
+            dma,
+        ] + [dma((peers,))] * 4
     mixed, returned = pl.pallas_call(
-        functools.partial(spectral_kernel, lat_n, lon_n),
+        functools.partial(kernel, lat_n, lon_n),
         out_shape=(
             jax.ShapeDtypeStruct((slots, degrees, 2 * channels), jnp.bfloat16),
             jax.ShapeDtypeStruct((queries, rows, channels), jnp.bfloat16),
         ),
         in_specs=[anywhere] + [vmem] * 5,
         out_specs=(vmem, anywhere),
-        scratch_shapes=[
-            pltpu.VMEM((rows, points, channels), jnp.bfloat16),
-            pltpu.VMEM((halves, queries * PITCH, LANES), jnp.float32),
-            pltpu.VMEM((queries, rows, channels), jnp.bfloat16),
-            pltpu.VMEM((2 * slots, peers + 1, rows, channels), jnp.bfloat16),
-            pltpu.VMEM((2 * slots, lat_n, rows, channels), jnp.bfloat16),
-            pltpu.SemaphoreType.DMA((rows // ROWS,)),
-            pltpu.SemaphoreType.DMA,
-            pltpu.SemaphoreType.DMA((peers,)),
-            pltpu.SemaphoreType.DMA((peers,)),
-            pltpu.SemaphoreType.DMA((peers,)),
-            pltpu.SemaphoreType.DMA((peers,)),
-        ],
+        scratch_shapes=scratch,
         compiler_params=pltpu.CompilerParams(
-            collective_id=0, has_side_effects=True, vmem_limit_bytes=60 * 1024 * 1024
+            collective_id=0, has_side_effects=True, vmem_limit_bytes=VMEM_BYTES
         ),
     )(field, table, analysis, synthesis, mixing[0], degree_gain[0])
     advanced = pl.pallas_call(
@@ -230,7 +434,7 @@
         ],
         out_specs=pl.BlockSpec((ROWS, points, channels), lambda i: (i, 0, 0)),
         scratch_shapes=[pltpu.VMEM((halves, queries * PITCH, LANES), jnp.float32)],
-        compiler_params=pltpu.CompilerParams(vmem_limit_bytes=60 * 1024 * 1024),
+        compiler_params=pltpu.CompilerParams(vmem_limit_bytes=VMEM_BYTES),
     )(field, returned, table.T, skip_weight[0])
     return advanced, mixed.reshape(slots, degrees, 2, channels)
 

time: 98.3 us -> 67.9 us (0.69)
  the two profiles are of different devices: /device:TPU:28 before, /device:TPU:1 now
where the time goes in v2:
time: 67.9 us; the launch traced here: 67.7 us
  Pallas kernels  63.8 us (94%)
  local copies, waits for them, and re-layouts  2.35 us (3%)
  other arithmetic  0.85 us (1%)
  between operations  0.68 us (1%)
    pallas_call x1, Pallas kernels, per_device(): pl.pallas_call(functools.partial(kernel, lat_n, lon_n), out_shape=(jax.Sh...  56.7 us
    pallas_call x1, Pallas kernels, per_device(): pl.pallas_call(grid_kernel, grid=(rows // ROWS,), out_shape=jax.ShapeDtyp...  7.12 us
    reshape x1, local copies, waits for them, and re-layouts, per_device(): return (advanced, mixed.reshape(slots, degrees, 2, channels))  1.61 us

profile of v2, /device:TPU:1, one launch (start us, length us, event | category | flops | bytes accessed | tf_op | source)
XLA Modules:
  0.0 67.7 jit_solution(10796167982017998410)
XLA Ops:
  0.6 0.8 %cosine_convert_fusion = (bf16[48,1,128]{2,0,1:T(8,128)(2,1)S(1)}, bf16[48,1,128]{2,0,1:T(8,128)(2,1)S(1)}) fusion(s32[128]{0:T(128)S(1)} %iota_add_fusion, s32[48]{0:T(128)} %param.8), kind=kLoop, calls=%fused_computation.10 | loop fusion | flops 104448 | bytes 25280 | tf_op jit(solution)/shard_map/convert
  1.5 0.0 copy-start
  1.5 0.7 %copy.12 = bf16[96,128]{0,1:T(8,128)(2,1)} copy(bf16[96,128]{1,0:T(8,128)(2,1)S(1)} %bitcast.6) | data formatting | bytes 49152 | tf_op jit(solution)/shard_map/convert_element_type | solution.py:24
  2.3 0.0 copy-done
  2.3 56.7 %shard_map.86 = (bf16[3,48,512]{2,1,0:T(8,128)(2,1)}, bf16[96,32,256]{2,1,0:T(8,128)(2,1)}) custom-call(bf16[32,128,256]{2,1,0:T(8,128)(2,1)} %field.3, bf16[96,128]{1,0:T(8,128)(2,1)} %bitcast.7, bf16[3,48,128]{2,1,0:T(8,128)(2,1)} %analysis.1, bf16[3,48,128]{2,1,0:T(8,128)(2,1)} %synthesis.1, bf16[2,256,256]{2,1,0:T(8,128)(2,1)} %bitcast.5, f32[48,256]{1,0:T(8,128)} %bitcast.10), custom_call_target="tpu_custom_call" | custom-call | tf_op jit(solution)/shard_map/pallas_call | solution.py:412
  59.0 1.6 %reshape.134 = bf16[3,48,2,256]{3,2,1,0:T(2,128)(2,1)} reshape(bf16[3,48,512]{2,1,0:T(8,128)(2,1)} %get-tuple-element.5) | data formatting | bytes 294912 | tf_op jit(solution)/shard_map/reshape | solution.py:439
  60.6 7.1 %shard_map.87 = bf16[32,128,256]{2,1,0:T(8,128)(2,1)} custom-call(bf16[32,128,256]{2,1,0:T(8,128)(2,1)} %field.3, bf16[96,32,256]{2,1,0:T(8,128)(2,1)} %get-tuple-element.4.returned, bf16[128,96]{1,0:T(8,128)(2,1)} %bitcast.8, bf16[256,256]{1,0:T(8,128)(2,1)} %bitcast.9), custom_call_target="tpu_custom_call" | custom-call | tf_op jit(solution)/shard_map/pallas_call | solution.py:425
  (3 shorter events, 0.0 us)
Async XLA Ops:
  1.5 0.7 %copy-start = (bf16[48,2,128]{2,1,0:T(2,128)(2,1)}, bf16[48,2,128]{2,1,0:T(2,128)(2,1)S(1)}, u32[]{:S(2)}) copy-start(bf16[48,2,128]{2,1,0:T(2,128)(2,1)S(1)} %copy.11) | copy-start | bytes 73732

commit v3 on v2

--- a/solution.py
+++ b/solution.py
@@ -158,9 +158,9 @@
     lat_n, lon_n,
     field, table, analysis, synthesis, mixing, gain,
     mixed, returned,
-    field_v, wide, outgoing, gathered, analysis_all, synthesis_all, part_out, part_in, mixed_all, made,
+    field_v, wide, outgoing, gathered, analysis_all, synthesis_all, part_out, part_in, mixed_all, made, landing, packed,
     load_sem, own_sem, table_send, table_recv, lat_send, lat_recv, lon_send, lon_recv,
-    mix_send, mix_recv, back_send, back_recv,
+    mix_send, mix_recv, back_send, back_recv, out_sem,
 ):
     lat = lax.axis_index("lat")
     lon = lax.axis_index("lon")
@@ -168,7 +168,10 @@
     slots, degrees, _ = analysis.shape
     per = 2 * slots
     all_rows = lat_n * rows
-    order = list(range(1, lon_n))[::-1] + [0]
+    order = sorted(range(1, lon_n), key=lambda k: abs(2 * k - lon_n)) + [0]
+    blocks = rows // ROWS
+    halves = channels // LANES
+    early = order[: lon_n // 2] if blocks > 1 else []
 
     def at_lat(a):
         return lax.rem(lat + a, lat_n)
@@ -197,43 +200,49 @@
             barrier, inc=1, device_id={"lat": to_lat, "lon": to_lon}, device_id_type=pl.DeviceIdType.MESH
         )
 
-    tables = []
-    transform = table[...]
-    for b in range(rows // ROWS):
-        loads[b].wait()
-        forward_rows(transform, field_v, wide, b)
-        if b == 0:
-            pl.semaphore_wait(barrier, len(peers))
-            for k in range(1, lon_n):
-                for t, (src, dst) in enumerate(((analysis, analysis_all), (synthesis, synthesis_all))):
-                    tables.append(
-                        remote(src, dst.at[k], table_send.at[t, k], table_recv.at[t, k], lat, at_lon(-k))
-                    )
-        relay_rows(wide, outgoing, b, lat_n, lon_n, per)
-
-    lat_copies = {}
-    for b in order:
+    def to_owners(b, part, index):
         target = at_lon(b)
-        own = pltpu.make_async_copy(outgoing.at[lat, target], gathered.at[b, :, lat], own_sem.at[b])
-        copies = [
+        return [
             remote(
-                outgoing.at[at_lat(a), target], gathered.at[b, :, lat],
-                lat_send.at[b, a], lat_recv.at[b, a], at_lat(a), lon,
+                outgoing.at[at_lat(a), target, :, part], gathered.at[b, :, lat, part],
+                lat_send.at[index, b, a], lat_recv.at[index, b, a], at_lat(a), lon,
             )
             for a in range(1, lat_n)
         ]
-        own.start()
-        lat_copies[b] = (own, copies)
+
+    tables = {}
+    lat_copies = {b: [] for b in order}
+    transform = table[...]
+    for b in range(blocks):
+        loads[b].wait()
+        slabs = wide.at[pl.ds(b * halves, halves)]
+        forward_rows(transform, field_v, slabs, b)
+        relay_rows(slabs, outgoing, b, lat_n, lon_n, per)
+        if b == 0:
+            pl.semaphore_wait(barrier, len(peers))
+        for k in early:
+            lat_copies[k] += to_owners(k, pl.ds(b * ROWS, ROWS), b)
+        if b == 0:
+            for t, (src, dst) in enumerate(((analysis, analysis_all), (synthesis, synthesis_all))):
+                for k in order[:-1]:
+                    tables[t, k] = remote(
+                        src, dst.at[k], table_send.at[t, k], table_recv.at[t, k], lat, at_lon(-k)
+                    )
+    owns = {}
+    for b in order:
+        if b not in early:
+            lat_copies[b] += to_owners(b, pl.ds(0, rows), 0)
+        owns[b] = pltpu.make_async_copy(outgoing.at[lat, at_lon(b)], gathered.at[b, :, lat], own_sem.at[b])
+        owns[b].start()
 
     lon_copies = []
     kept = []
     for b in order:
-        own, copies = lat_copies[b]
-        own.wait()
-        for copy in copies:
+        owns[b].wait()
+        for copy in lat_copies[b]:
             copy.wait_recv()
         if b:
-            tables[2 * (b - 1)].wait_recv()
+            tables[0, b].wait_recv()
         for s in range(slots):
             weights = analysis_all[b, s] if b else analysis[s]
             for r in range(2):
@@ -264,45 +273,70 @@
         mixed[s, :, :channels] = real.astype(jnp.bfloat16)
         mixed[s, :, channels:] = imag.astype(jnp.bfloat16)
 
+    back_order = order[::-1]
     mix_copies = {
         b: remote(mixed, mixed_all.at[b], mix_send.at[b], mix_recv.at[b], lat, at_lon(-b))
-        for b in range(1, lon_n)
+        for b in back_order[1:]
     }
-    backs = []
-    owns = []
-    for b in range(lon_n):
+    backs = {}
+    for b in back_order:
         if b:
             mix_copies[b].wait_recv()
-            tables[2 * (b - 1) + 1].wait_recv()
+            tables[1, b].wait_recv()
         for s in range(slots):
             weights = synthesis_all[b, s] if b else synthesis[s]
             values = dot_t(weights, mixed_all[b, s] if b else mixed[s]).astype(jnp.bfloat16)
             for r in range(2):
                 for a in range(lat_n):
                     made[a, b, 2 * s + r] = values[a * rows : (a + 1) * rows, r * channels : (r + 1) * channels]
-        spot = pl.ds((lat * lon_n + at_lon(b)) * per, per)
         for a in range(1, lat_n):
-            backs.append(
-                remote(
-                    made.at[at_lat(a), b], returned.at[spot],
-                    back_send.at[b, a], back_recv.at[b, a], at_lat(a), lon,
-                )
+            backs[b, a] = remote(
+                made.at[at_lat(a), b], landing.at[b, a],
+                back_send.at[b, a], back_recv.at[b, a], at_lat(a), lon,
             )
-        own = pltpu.make_async_copy(made.at[lat, b], returned.at[spot], own_sem.at[b])
-        own.start()
-        owns.append(own)
-    for own in owns:
-        own.wait()
-    for copy in tables + [c for b in order for c in lat_copies[b][1]] + lon_copies + list(mix_copies.values()):
+        owns[b] = pltpu.make_async_copy(made.at[lat, b], landing.at[b, 0], own_sem.at[b])
+        owns[b].start()
+
+    for b in back_order:
+        owns[b].wait()
+        for a in range(1, lat_n):
+            backs[b, a].wait_recv()
+        for a in range(lat_n):
+            source = at_lat(lat_n - a) * lon_n + at_lon(b)
+            base = pl.multiple_of(source * (per * PITCH), 8)
+            for i in range(per):
+                values = landing[b, a, i].astype(jnp.float32)
+                for c in range(blocks):
+                    for h in range(halves):
+                        wide[c * halves + h, pl.ds(base + i * PITCH, ROWS), :] = values[
+                            c * ROWS : (c + 1) * ROWS, h * LANES : (h + 1) * LANES
+                        ]
+
+    queries = table.shape[0]
+    outs = []
+    for c in range(blocks):
+
+        @pl.loop(0, ROWS, unroll=4)
+        def _(j):
+            for h in range(halves):
+                packed[c * ROWS + j, :, h * LANES : (h + 1) * LANES] = wide.at[c * halves + h][
+                    pl.ds(j, queries, stride=PITCH), :
+                ].astype(jnp.bfloat16)
+
+        part = pl.ds(c * ROWS, ROWS)
+        outs.append(pltpu.make_async_copy(packed.at[part], returned.at[part], out_sem.at[c]))
+        outs[-1].start()
+    for copy in outs:
+        copy.wait()
+    sent = list(tables.values()) + [c for b in order for c in lat_copies[b]] + lon_copies
+    for copy in sent + list(mix_copies.values()) + list(backs.values()):
         copy.wait_send()
-    for copy in backs:
-        copy.wait()
 
 
 def forward_rows(transform, field_v, wide, b):
     queries = transform.shape[0]
 
-    @pl.loop(0, ROWS, unroll=2)
+    @pl.loop(0, ROWS, unroll=4)
     def _(j):
         y = dot(transform, field_v[b * ROWS + j])
         for h in range(wide.shape[0]):
@@ -354,6 +388,27 @@
         out[j] = (state.astype(jnp.float32) + gelu(pre)).astype(jnp.bfloat16)
 
 
+def packed_grid_kernel(field, returned, table, skip, mixed, out, spectrum, table_t):
+    rows, points, channels = field.shape
+
+    @pl.when(pl.program_id(0) == 0)
+    def _():
+        table_t[...] = table[...].astype(jnp.float32).T.astype(jnp.bfloat16)
+        for s in range(mixed.shape[0]):
+            both = mixed[s].astype(jnp.float32)
+            spectrum[s] = jnp.stack([both[:, :channels], both[:, channels:]], axis=1).astype(jnp.bfloat16)
+
+    transform = table_t[...]
+    weights = skip[...]
+
+    @pl.loop(0, rows, unroll=4)
+    def _(j):
+        spectral = dot(transform, returned[j]).astype(jnp.bfloat16).astype(jnp.float32)
+        state = field[j]
+        pre = spectral + dot(state, weights)
+        out[j] = (state.astype(jnp.float32) + gelu(pre)).astype(jnp.bfloat16)
+
+
 def per_device(lat_n, lon_n, field, mode_table, analysis, synthesis, mixing, degree_gain, skip_weight):
     rows, points, channels = field.shape
     modes = mode_table.shape[0]
@@ -364,7 +419,8 @@
     vmem = pl.BlockSpec(memory_space=pltpu.VMEM)
     anywhere = pl.BlockSpec(memory_space=pl.ANY)
     halves = channels // LANES
-    wide = pltpu.VMEM((halves, queries * PITCH, LANES), jnp.float32)
+    wide_shape = (halves, queries * PITCH, LANES)
+    blocks = rows // ROWS
     exchanged = (lat_n, lon_n, 2 * slots, rows, channels)
     coded = (lon_n, slots, degrees, 2 * channels)
     weights = (lon_n,) + analysis.shape
@@ -378,31 +434,35 @@
         (coded, jnp.bfloat16),
         (coded, jnp.bfloat16),
         (exchanged, jnp.bfloat16),
+        ((lon_n, lat_n, 2 * slots, rows, channels), jnp.bfloat16),
+        ((rows, queries, channels), jnp.bfloat16),
     ]
-    held = sum(2 * math.prod(shape) for shape, _ in staged) + 4 * halves * queries * PITCH * LANES
+    held = sum(2 * math.prod(shape) for shape, _ in staged) + 4 * blocks * math.prod(wide_shape)
+    fits = held < VMEM_BYTES * 3 // 4
     dma = pltpu.SemaphoreType.DMA
-    if held < VMEM_BYTES * 3 // 4:
+    if fits:
         kernel = staged_kernel
         buffers = [pltpu.VMEM(shape, dtype) for shape, dtype in staged]
-        scratch = [buffers[0], wide] + buffers[1:] + [
+        scratch = [buffers[0], pltpu.VMEM((blocks * halves,) + wide_shape[1:], jnp.float32)] + buffers[1:] + [
             dma((rows // ROWS,)),
             dma((lon_n,)),
             dma((2, lon_n)),
             dma((2, lon_n)),
-            dma((lon_n, lat_n)),
-            dma((lon_n, lat_n)),
+            dma((blocks, lon_n, lat_n)),
+            dma((blocks, lon_n, lat_n)),
             dma((lon_n,)),
             dma((lon_n,)),
             dma((lon_n,)),
             dma((lon_n,)),
             dma((lon_n, lat_n)),
             dma((lon_n, lat_n)),
+            dma((blocks,)),
         ]
     else:
         kernel = spectral_kernel
         scratch = [
             pltpu.VMEM((rows, points, channels), jnp.bfloat16),
-            wide,
+            pltpu.VMEM(wide_shape, jnp.float32),
             pltpu.VMEM((queries, rows, channels), jnp.bfloat16),
             pltpu.VMEM((2 * slots, peers + 1, rows, channels), jnp.bfloat16),
             pltpu.VMEM((2 * slots, lat_n, rows, channels), jnp.bfloat16),
@@ -413,7 +473,7 @@
         functools.partial(kernel, lat_n, lon_n),
         out_shape=(
             jax.ShapeDtypeStruct((slots, degrees, 2 * channels), jnp.bfloat16),
-            jax.ShapeDtypeStruct((queries, rows, channels), jnp.bfloat16),
+            jax.ShapeDtypeStruct((rows, queries, channels) if fits else (queries, rows, channels), jnp.bfloat16),
         ),
         in_specs=[anywhere] + [vmem] * 5,
         out_specs=(vmem, anywhere),
@@ -422,6 +482,28 @@
             collective_id=0, has_side_effects=True, vmem_limit_bytes=VMEM_BYTES
         ),
     )(field, table, analysis, synthesis, mixing[0], degree_gain[0])
+    if fits:
+        step = ROWS // 2
+        whole = lambda shape: pl.BlockSpec(shape, lambda i: (0,) * len(shape))
+        spectrum = (slots, degrees, 2, channels)
+        return pl.pallas_call(
+            packed_grid_kernel,
+            grid=(rows // step,),
+            out_shape=(
+                jax.ShapeDtypeStruct(field.shape, jnp.bfloat16),
+                jax.ShapeDtypeStruct(spectrum, jnp.bfloat16),
+            ),
+            in_specs=[
+                pl.BlockSpec((step, points, channels), lambda i: (i, 0, 0)),
+                pl.BlockSpec((step, queries, channels), lambda i: (i, 0, 0)),
+                whole(table.shape),
+                whole((channels, channels)),
+                whole(mixed.shape),
+            ],
+            out_specs=(pl.BlockSpec((step, points, channels), lambda i: (i, 0, 0)), whole(spectrum)),
+            scratch_shapes=[pltpu.VMEM((points, queries), jnp.bfloat16)],
+            compiler_params=pltpu.CompilerParams(vmem_limit_bytes=VMEM_BYTES),
+        )(field, returned, table, skip_weight[0], mixed)
     advanced = pl.pallas_call(
         grid_kernel,
         grid=(rows // ROWS,),
@@ -433,7 +515,7 @@
             pl.BlockSpec((channels, channels), lambda i: (0, 0)),
         ],
         out_specs=pl.BlockSpec((ROWS, points, channels), lambda i: (i, 0, 0)),
-        scratch_shapes=[pltpu.VMEM((halves, queries * PITCH, LANES), jnp.float32)],
+        scratch_shapes=[pltpu.VMEM(wide_shape, jnp.float32)],
         compiler_params=pltpu.CompilerParams(vmem_limit_bytes=VMEM_BYTES),
     )(field, returned, table.T, skip_weight[0])
     return advanced, mixed.reshape(slots, degrees, 2, channels)

time: 67.9 us -> 60.4 us (0.89)
  Pallas kernels: 63.8 us -> 58 us
  local copies, waits for them, and re-layouts: 2.35 us -> 0.63 us
    pallas_call x1, Pallas kernels: 56.7 us -> 52.1 us  [per_device(): pl.pallas_call(functools.partial(kernel, lat_n, lon_n), out_shape=(jax.Sh...]
    reshape x1 -> x0, local copies, waits for them, and re-layouts: 1.61 us -> none  [per_device(): return (advanced, mixed.reshape(slots, degrees, 2, channels))]
    pallas_call x1, Pallas kernels: 7.12 us -> 5.95 us  [per_device(): pl.pallas_call(packed_grid_kernel, grid=(rows // step,), out_shape=(jax.S...]
    convert_element_type x1 -> x0, local copies, waits for them, and re-layouts: 0.71 us -> none  [fourier_table(): return jnp.stack([jnp.cos(angles), -jnp.sin(angles)], axis=1).reshape(2 *...]
where the time goes in v3:
time: 60.4 us; the launch traced here: 60.2 us
  Pallas kernels  58 us (96%)
  other arithmetic  0.85 us (1%)
  between operations  0.66 us (1%)
  local copies, waits for them, and re-layouts  0.63 us (1%)
    pallas_call x1, Pallas kernels, per_device(): pl.pallas_call(functools.partial(kernel, lat_n, lon_n), out_shape=(jax.Sh...  52.1 us
    pallas_call x1, Pallas kernels, per_device(): pl.pallas_call(packed_grid_kernel, grid=(rows // step,), out_shape=(jax.S...  5.95 us

profile of v3, /device:TPU:1, one launch (start us, length us, event | category | flops | bytes accessed | tf_op | source)
XLA Modules:
  0.0 60.2 jit_solution(13840191944268628476)
XLA Ops:
  0.6 0.8 %cosine_convert_fusion = (bf16[48,1,128]{2,0,1:T(8,128)(2,1)S(1)}, bf16[48,1,128]{2,0,1:T(8,128)(2,1)S(1)}) fusion(s32[128]{0:T(128)S(1)} %iota_add_fusion, s32[48]{0:T(128)} %param.8), kind=kLoop, calls=%fused_computation.10 | loop fusion | flops 104448 | bytes 25280 | tf_op jit(solution)/shard_map/convert
  1.5 0.6 %copy.9 = bf16[48,2,128]{2,1,0:T(2,128)(2,1)} copy(bf16[48,2,128]{2,0,1:T(8,128)(2,1)S(1)} %pad_maximum_fusion) | data formatting | bytes 49152 | tf_op jit(solution)/shard_map/stack | solution.py:22
  2.1 52.1 %shard_map.86 = (bf16[3,48,512]{2,1,0:T(8,128)(2,1)}, bf16[32,96,256]{2,1,0:T(8,128)(2,1)}) custom-call(bf16[32,128,256]{2,1,0:T(8,128)(2,1)} %field.3, bf16[96,128]{1,0:T(8,128)(2,1)} %bitcast.5, bf16[3,48,128]{2,1,0:T(8,128)(2,1)} %analysis.1, bf16[3,48,128]{2,1,0:T(8,128)(2,1)} %synthesis.1, bf16[2,256,256]{2,1,0:T(8,128)(2,1)} %bitcast.4, f32[48,256]{1,0:T(8,128)} %bitcast.8), custom_call_target="tpu_custom_call" | custom-call | tf_op jit(solution)/shard_map/pallas_call | solution.py:472
  54.2 6.0 %shard_map.87 = (bf16[32,128,256]{2,1,0:T(8,128)(2,1)}, bf16[3,48,2,256]{3,2,1,0:T(2,128)(2,1)}) custom-call(bf16[32,128,256]{2,1,0:T(8,128)(2,1)} %field.3, bf16[32,96,256]{2,1,0:T(8,128)(2,1)} %get-tuple-element.4.returned, bf16[96,128]{1,0:T(8,128)(2,1)} %bitcast.6, bf16[256,256]{1,0:T(8,128)(2,1)} %bitcast.7, bf16[3,48,512]{2,1,0:T(8,128)(2,1)} %get-tuple-element.5.mixed), custom_call_target="tpu_custom_call" | custom-call | tf_op jit(solution)/shard_map/pallas_call | solution.py:489
  (2 shorter events, 0.0 us)

commit v4 on v3

--- a/solution.py
+++ b/solution.py
@@ -16,13 +16,13 @@
 
 def fourier_table(orders, first, count, length):
     points = first + jnp.arange(count, dtype=jnp.int32)
-    phases = orders[:, None] * points[None, :] % length
-    angles = phases.astype(jnp.float32) * (2.0 * math.pi / length)
-    return (
-        jnp.stack([jnp.cos(angles), -jnp.sin(angles)], axis=1)
-        .reshape(2 * orders.shape[0], count)
-        .astype(jnp.bfloat16)
-    )
+    if length % 4:
+        angles = (orders[:, None] * points[None, :] % length).astype(jnp.float32) * (2.0 * math.pi / length)
+        both = jnp.stack([jnp.cos(angles), -jnp.sin(angles)], axis=1)
+        return both.reshape(2 * orders.shape[0], count).astype(jnp.bfloat16)
+    quarter = (jnp.arange(2 * orders.shape[0], dtype=jnp.int32) % 2) * (length // 4)
+    phases = (jnp.repeat(orders, 2)[:, None] * points[None, :] + quarter[:, None]) % length
+    return jnp.cos(phases.astype(jnp.float32) * (2.0 * math.pi / length)).astype(jnp.bfloat16)
 
 
 def dot(a, b):
@@ -273,34 +273,81 @@
         mixed[s, :, :channels] = real.astype(jnp.bfloat16)
         mixed[s, :, channels:] = imag.astype(jnp.bfloat16)
 
-    back_order = order[::-1]
-    mix_copies = {
-        b: remote(mixed, mixed_all.at[b], mix_send.at[b], mix_recv.at[b], lat, at_lon(-b))
-        for b in back_order[1:]
-    }
-    backs = {}
-    for b in back_order:
-        if b:
-            mix_copies[b].wait_recv()
-            tables[1, b].wait_recv()
+    def mix_copy(src, k, send, to_lon):
+        return pltpu.make_async_remote_copy(
+            src_ref=src, dst_ref=mixed_all.at[k], send_sem=mix_send.at[send], recv_sem=mix_recv.at[k],
+            device_id={"lat": lat, "lon": to_lon}, device_id_type=pl.DeviceIdType.MESH,
+        )
+
+    def onward(k, step):
+        if k == 0:
+            return mix_copy(mixed, 1 if step < 0 else lon_n - 1, 0 if step < 0 else lon_n, at_lon(step))
+        return mix_copy(mixed_all.at[k], k - step, k, at_lon(step))
+
+    def back_copy(k, a):
+        return pltpu.make_async_remote_copy(
+            src_ref=made.at[at_lat(a), k], dst_ref=landing.at[k, a],
+            send_sem=back_send.at[k, a], recv_sem=back_recv.at[k, a],
+            device_id={"lat": at_lat(a), "lon": lon}, device_id_type=pl.DeviceIdType.MESH,
+        )
+
+    def own_copy(k):
+        return pltpu.make_async_copy(made.at[lat, k], landing.at[k, 0], own_sem.at[k])
+
+    def emit(k):
         for s in range(slots):
-            weights = synthesis_all[b, s] if b else synthesis[s]
-            values = dot_t(weights, mixed_all[b, s] if b else mixed[s]).astype(jnp.bfloat16)
+            weights = synthesis_all[k, s] if k else synthesis[s]
+            values = dot_t(weights, mixed_all[k, s] if k else mixed[s]).astype(jnp.bfloat16)
             for r in range(2):
                 for a in range(lat_n):
-                    made[a, b, 2 * s + r] = values[a * rows : (a + 1) * rows, r * channels : (r + 1) * channels]
+                    made[a, k, 2 * s + r] = values[a * rows : (a + 1) * rows, r * channels : (r + 1) * channels]
         for a in range(1, lat_n):
-            backs[b, a] = remote(
-                made.at[at_lat(a), b], landing.at[b, a],
-                back_send.at[b, a], back_recv.at[b, a], at_lat(a), lon,
-            )
-        owns[b] = pltpu.make_async_copy(made.at[lat, b], landing.at[b, 0], own_sem.at[b])
-        owns[b].start()
-
+            back_copy(k, a).start()
+        own_copy(k).start()
+
+    has_right = lon < lon_n - 1
+    has_left = lon > 0
+
+    @pl.when(has_right)
+    def _():
+        onward(0, 1).start()
+
+    @pl.when(has_left)
+    def _():
+        onward(0, -1).start()
+
+    emit(0)
+    for k in order[:-1]:
+        tables[1, k].wait_recv()
+    for d in range(1, lon_n):
+
+        @pl.when(lon >= d)
+        def _():
+            mix_copy(mixed, lon_n - d, lon_n - d, at_lon(1)).wait_recv()
+            if d < lon_n - 1:
+
+                @pl.when(has_right)
+                def _():
+                    onward(lon_n - d, 1).start()
+
+            emit(lon_n - d)
+
+        @pl.when(lon + d < lon_n)
+        def _():
+            mix_copy(mixed, d, d, at_lon(1)).wait_recv()
+            if d < lon_n - 1:
+
+                @pl.when(has_left)
+                def _():
+                    onward(d, -1).start()
+
+            emit(d)
+
+    back_order = [0] + sorted(range(1, lon_n), key=lambda k: -abs(2 * k - lon_n))
     for b in back_order:
-        owns[b].wait()
+        own_copy(b).wait()
         for a in range(1, lat_n):
-            backs[b, a].wait_recv()
+            back_copy(b, a).wait_recv()
         for a in range(lat_n):
             source = at_lat(lat_n - a) * lon_n + at_lon(b)
             base = pl.multiple_of(source * (per * PITCH), 8)
@@ -329,8 +376,26 @@
     for copy in outs:
         copy.wait()
     sent = list(tables.values()) + [c for b in order for c in lat_copies[b]] + lon_copies
-    for copy in sent + list(mix_copies.values()) + list(backs.values()):
+    for copy in sent + [back_copy(b, a) for b in range(lon_n) for a in range(1, lat_n)]:
         copy.wait_send()
+
+    @pl.when(has_right)
+    def _():
+        onward(0, 1).wait_send()
+
+    @pl.when(has_left)
+    def _():
+        onward(0, -1).wait_send()
+
+    for d in range(1, lon_n - 1):
+
+        @pl.when((lon >= d) & has_right)
+        def _():
+            onward(lon_n - d, 1).wait_send()
+
+        @pl.when((lon + d < lon_n) & has_left)
+        def _():
+            onward(d, -1).wait_send()
 
 
 def forward_rows(transform, field_v, wide, b):
@@ -452,7 +517,7 @@
             dma((blocks, lon_n, lat_n)),
             dma((lon_n,)),
             dma((lon_n,)),
-            dma((lon_n,)),
+            dma((lon_n + 1,)),
             dma((lon_n,)),
             dma((lon_n, lat_n)),
             dma((lon_n, lat_n)),

time: 60.4 us -> 61.1 us (1.012)
    convert_element_type x0 -> x1, other arithmetic: none -> 0.88 us  [fourier_table(): jnp.cos(phases.astype(jnp.float32) * (2.0 * math.pi / length))]
    another operation x2 -> x0, other arithmetic: 0.85 us -> none
    broadcast_in_dim x0 -> x1, local copies, waits for them, and re-layouts: none -> 0.73 us  [fourier_table(): jnp.repeat(orders, 2)[:, None] * points[None, :] + quarter[:, None]]
    another operation x1 -> x0, local copies, waits for them, and re-layouts: 0.63 us -> none  [fourier_table(): jnp.stack([jnp.cos(angles), -jnp.sin(angles)], axis=1)]
where the time goes in v4:
time: 61.1 us; the launch traced here: 60.8 us
  Pallas kernels  58.4 us (96%)
  other arithmetic  0.89 us (1%)
  local copies, waits for them, and re-layouts  0.85 us (1%)
  between operations  0.66 us (1%)
    pallas_call x1, Pallas kernels, per_device(): pl.pallas_call(functools.partial(kernel, lat_n, lon_n), out_shape=(jax.Sh...  52.4 us
    pallas_call x1, Pallas kernels, per_device(): pl.pallas_call(packed_grid_kernel, grid=(rows // step,), out_shape=(jax.S...  5.96 us

profile of v4, /device:TPU:1, one launch (start us, length us, event | category | flops | bytes accessed | tf_op | source)
XLA Modules:
  0.0 60.8 jit_solution(15855286478345125907)
XLA Ops:
  0.7 0.7 %broadcast_in_dim.2 = s32[48,2]{1,0:T(8,128)S(1)} broadcast(s32[48]{0:T(128)} %param.8), dimensions={0} | broadcast | bytes 576 | tf_op jit(solution)/shard_map/broadcast_in_dim | solution.py:24
  1.4 0.1 mul.34
  1.5 0.9 %fusion.4.table = bf16[96,128]{1,0:T(8,128)(2,1)} fusion(s32[96]{0:T(128)S(1)} %fusion.5, s32[128]{0:T(128)S(1)} %iota_add_fusion, s32[96]{0:T(128)S(1)} %mul.34), kind=kLoop, calls=%fused_computation.7 | loop fusion | flops 196608 | bytes 25856 | tf_op jit(solution)/shard_map/convert_element_type | solution.py:25
  2.4 52.4 %shard_map.86 = (bf16[3,48,512]{2,1,0:T(8,128)(2,1)}, bf16[32,96,256]{2,1,0:T(8,128)(2,1)}) custom-call(bf16[32,128,256]{2,1,0:T(8,128)(2,1)} %field.3, bf16[96,128]{1,0:T(8,128)(2,1)} %fusion.4.table, bf16[3,48,128]{2,1,0:T(8,128)(2,1)} %analysis.1, bf16[3,48,128]{2,1,0:T(8,128)(2,1)} %synthesis.1, bf16[2,256,256]{2,1,0:T(8,128)(2,1)} %bitcast.3, ...), custom_call_target="tpu_custom_call" | custom-call | tf_op jit(solution)/shard_map/pallas_call | solution.py:537
  54.8 6.0 %shard_map.87 = (bf16[32,128,256]{2,1,0:T(8,128)(2,1)}, bf16[3,48,2,256]{3,2,1,0:T(2,128)(2,1)}) custom-call(bf16[32,128,256]{2,1,0:T(8,128)(2,1)} %field.3, bf16[32,96,256]{2,1,0:T(8,128)(2,1)} %get-tuple-element.4.returned, bf16[96,128]{1,0:T(8,128)(2,1)} %fusion.4.table, bf16[256,256]{1,0:T(8,128)(2,1)} %bitcast.4, bf16[3,48,512]{2,1,0:T(8,128)(2,1)} %get-tuple-element.5.mixed), custom_call_target="tpu_custom_call" | custom-call | tf_op jit(solution)/shard_map/pallas_call | solution.py:554
  (2 shorter events, 0.0 us)

commit v5 on v3

--- a/solution.py
+++ b/solution.py
@@ -261,6 +261,23 @@
     real_w = mixing[0]
     imag_w = mixing[1]
     gains = gain[...]
+    back_order = order[::-1]
+    mix_copies = {}
+    backs = {}
+
+    def emit(b, s):
+        weights = synthesis_all[b, s] if b else synthesis[s]
+        values = dot_t(weights, mixed_all[b, s] if b else mixed[s]).astype(jnp.bfloat16)
+        for r in range(2):
+            for a in range(lat_n):
+                made[a, b, 2 * s + r] = values[a * rows : (a + 1) * rows, r * channels : (r + 1) * channels]
+        part = pl.ds(2 * s, 2)
+        for a in range(1, lat_n):
+            backs[b, s, a] = remote(
+                made.at[at_lat(a), b, part], landing.at[b, a, part],
+                back_send.at[b * slots + s, a], back_recv.at[b * slots + s, a], at_lat(a), lon,
+            )
+
     for s in range(slots):
         parts = []
         for r in range(2):
@@ -272,35 +289,26 @@
         imag = (dot(parts[0], imag_w) + dot(parts[1], real_w)) * gains
         mixed[s, :, :channels] = real.astype(jnp.bfloat16)
         mixed[s, :, channels:] = imag.astype(jnp.bfloat16)
-
-    back_order = order[::-1]
-    mix_copies = {
-        b: remote(mixed, mixed_all.at[b], mix_send.at[b], mix_recv.at[b], lat, at_lon(-b))
-        for b in back_order[1:]
-    }
-    backs = {}
+        for b in back_order[1:]:
+            n = b * slots + s
+            mix_copies[b, s] = remote(
+                mixed.at[s], mixed_all.at[b, s], mix_send.at[n], mix_recv.at[n], lat, at_lon(-b)
+            )
+        emit(0, s)
     for b in back_order:
         if b:
-            mix_copies[b].wait_recv()
             tables[1, b].wait_recv()
-        for s in range(slots):
-            weights = synthesis_all[b, s] if b else synthesis[s]
-            values = dot_t(weights, mixed_all[b, s] if b else mixed[s]).astype(jnp.bfloat16)
-            for r in range(2):
-                for a in range(lat_n):
-                    made[a, b, 2 * s + r] = values[a * rows : (a + 1) * rows, r * channels : (r + 1) * channels]
-        for a in range(1, lat_n):
-            backs[b, a] = remote(
-                made.at[at_lat(a), b], landing.at[b, a],
-                back_send.at[b, a], back_recv.at[b, a], at_lat(a), lon,
-            )
+            for s in range(slots):
+                mix_copies[b, s].wait_recv()
+                emit(b, s)
         owns[b] = pltpu.make_async_copy(made.at[lat, b], landing.at[b, 0], own_sem.at[b])
         owns[b].start()
 
     for b in back_order:
         owns[b].wait()
         for a in range(1, lat_n):
-            backs[b, a].wait_recv()
+            for s in range(slots):
+                backs[b, s, a].wait_recv()
         for a in range(lat_n):
             source = at_lat(lat_n - a) * lon_n + at_lon(b)
             base = pl.multiple_of(source * (per * PITCH), 8)
@@ -452,10 +460,10 @@
             dma((blocks, lon_n, lat_n)),
             dma((lon_n,)),
             dma((lon_n,)),
-            dma((lon_n,)),
-            dma((lon_n,)),
-            dma((lon_n, lat_n)),
-            dma((lon_n, lat_n)),
+            dma((lon_n * slots,)),
+            dma((lon_n * slots,)),
+            dma((lon_n * slots, lat_n)),
+            dma((lon_n * slots, lat_n)),
             dma((blocks,)),
         ]
     else:

time: 60.4 us -> 63.9 us (1.058)
  the two profiles are of different devices: /device:TPU:1 before, /device:TPU:19 now
where the time goes in v5:
time: 63.9 us; the launch traced here: 63.6 us
  Pallas kernels  61.5 us (96%)
  other arithmetic  0.85 us (1%)
  between operations  0.66 us (1%)
    pallas_call x1, Pallas kernels, per_device(): pl.pallas_call(functools.partial(kernel, lat_n, lon_n), out_shape=(jax.Sh...  55.5 us
    pallas_call x1, Pallas kernels, per_device(): pl.pallas_call(packed_grid_kernel, grid=(rows // step,), out_shape=(jax.S...  5.96 us

profile of v5, /device:TPU:19, one launch (start us, length us, event | category | flops | bytes accessed | tf_op | source)
XLA Modules:
  0.0 63.6 jit_solution(4546414333393550669)
XLA Ops:
  0.6 0.8 %cosine_convert_fusion = (bf16[48,1,128]{2,0,1:T(8,128)(2,1)S(1)}, bf16[48,1,128]{2,0,1:T(8,128)(2,1)S(1)}) fusion(s32[128]{0:T(128)S(1)} %iota_add_fusion, s32[48]{0:T(128)} %param.8), kind=kLoop, calls=%fused_computation.10 | loop fusion | flops 104448 | bytes 25280 | tf_op jit(solution)/shard_map/convert
  1.5 0.6 copy.9
  2.1 55.5 %shard_map.86 = (bf16[3,48,512]{2,1,0:T(8,128)(2,1)}, bf16[32,96,256]{2,1,0:T(8,128)(2,1)}) custom-call(bf16[32,128,256]{2,1,0:T(8,128)(2,1)} %field.3, bf16[96,128]{1,0:T(8,128)(2,1)} %bitcast.5, bf16[3,48,128]{2,1,0:T(8,128)(2,1)} %analysis.1, bf16[3,48,128]{2,1,0:T(8,128)(2,1)} %synthesis.1, bf16[2,256,256]{2,1,0:T(8,128)(2,1)} %bitcast.4, f32[48,256]{1,0:T(8,128)} %bitcast.8), custom_call_target="tpu_custom_call" | custom-call | tf_op jit(solution)/shard_map/pallas_call | solution.py:480
  57.6 6.0 %shard_map.87 = (bf16[32,128,256]{2,1,0:T(8,128)(2,1)}, bf16[3,48,2,256]{3,2,1,0:T(2,128)(2,1)}) custom-call(bf16[32,128,256]{2,1,0:T(8,128)(2,1)} %field.3, bf16[32,96,256]{2,1,0:T(8,128)(2,1)} %get-tuple-element.4.returned, bf16[96,128]{1,0:T(8,128)(2,1)} %bitcast.6, bf16[256,256]{1,0:T(8,128)(2,1)} %bitcast.7, bf16[3,48,512]{2,1,0:T(8,128)(2,1)} %get-tuple-element.5.mixed), custom_call_target="tpu_custom_call" | custom-call | tf_op jit(solution)/shard_map/pallas_call | solution.py:497
  (2 shorter events, 0.0 us)
